TPU v7x, 128 devices: a whole 4x4x4 slice. The times are simulated.
128 devices in a mesh: prow: 4 (over x), pcol: 32 (over z, y, core).
Axes of the slice: x: 4, y: 4, z: 4, core: 2. Of those that a mesh axis runs over, the one named last changes fastest.
Arguments:
- match_tiles: float32 [128, 8, 128, 128], P('pcol', 'prow'), may hold values from 0.05 to 1
- pattern: int32 [128, 8], replicated, may hold values from 0 to 127, as said below
- kept: int32 [128, 8], replicated, may hold values from 0 to 127, as said below
- panel_order: int32 [32], replicated, may hold values from 0 to 31, as said below
Outputs:
- clusters: float32 [128, 8, 128, 128], P('pcol', 'prow')
Inputs may be any that keep to these rules, and one draw needn't show every extreme that they name: `pattern`: slots r * 2 to r * 2 + 1 of a tile column name 2 different tile rows of the r-th of the equal row blocks along prow. Tile column j names itself and tile column j + 1 - 2 * (j % 2) in the row block that holds tile row j. Of the tile columns of one panel, the tile columns of any other panel name at most 1 different ones, and exactly 1 for some pairs of panels. `kept`: as for pattern, with the same 1; every named tile is nonzero in the product of the input matrix with itself. `panel_order`: A permutation in which every entry differs from its index by at most one.
All inputs are finite; a program needn't handle non-finite values.
Results may differ from a plain program's by a relative error of at most 0.0003.
Values sent between devices are 32-bit elements; how exact they have to be, the bound alone decides.
No kernel may reach another device: no remote copies, remote signals or barrier semaphores. Data moves between devices by JAX's collectives and lax.ppermute only.
A program may use at most 64 MiB of HBM per device.

v0:
```python
import jax
import jax.numpy as jnp
from jax import lax
from jax.sharding import PartitionSpec as P


def copy_for_each(x, axis):
    length = lax.axis_size(axis)
    return lax.all_to_all(jnp.broadcast_to(x[None], (length, *x.shape)), axis, 0, 0, tiled=True)


def of_everyone(x, axis):
    everything = copy_for_each(x, axis)
    return jnp.sum(everything, axis=0)


def joined_along(tiles, dim):
    shape = list(tiles.shape[1:])
    shape[dim] *= tiles.shape[0]
    return jnp.moveaxis(tiles, 0, dim).reshape(shape)


def gather_directly(x, axis, dim):
    tiles = copy_for_each(x, axis)
    return joined_along(tiles, dim)


def column_partial(row_block):
    return jnp.sum(row_block, axis=(1, 2))


def sum_columns(partial_value):
    return of_everyone(partial_value, "prow")


def gather_pieces_together(row_block, want_whole):
    partial_value = column_partial(row_block)
    whole_cols = None
    totals = sum_columns(partial_value)
    normal = row_block / totals[:, None, None, :]
    if want_whole:
        whole_cols = gather_directly(normal, "prow", 1)
    return (whole_cols, normal)


def locate(column_ids, wanted):
    matches = column_ids[None, None, :] == wanted[:, :, None]
    counter = jnp.arange(column_ids.shape[0], dtype=jnp.int32)
    return jnp.sum(jnp.where(matches, counter[None, None, :], 0), axis=-1)


def strip_table(normal):
    tile_table = lax.all_gather(normal, "pcol", axis=0, tiled=True)
    column_ids = jnp.arange(tile_table.shape[0], dtype=jnp.int32)
    return (tile_table, column_ids)


def multiply(
    tile_table, column_ids, in_pattern, out_pattern, whole_cols, panel_at, row_index, block_share
):
    panel_cols = whole_cols.shape[0]
    named_refs = lax.dynamic_slice_in_dim(in_pattern, panel_at * panel_cols, panel_cols, 0)
    positions = locate(column_ids, named_refs)
    block_rows = lax.dynamic_slice_in_dim(in_pattern, row_index * block_share, block_share, 1)
    table_rows = block_rows[jnp.clip(column_ids, 0, block_rows.shape[0] - 1)]
    needed = tile_table[positions]
    needed_rows = table_rows[positions]
    wanted = lax.dynamic_slice(
        out_pattern, (panel_at * panel_cols, row_index * block_share), (panel_cols, block_share)
    )
    weights = (needed_rows[:, None, :, :] == wanted[:, :, None, None]).astype(jnp.float32)
    selected_entries = jnp.einsum(
        "jtks,jksab->jtkab", weights, needed, precision=lax.Precision.HIGHEST
    )
    return jnp.einsum(
        "jtkab,jkbc->jtac", selected_entries, whole_cols, precision=lax.Precision.HIGHEST
    )


def local(match_tiles, pattern, kept, panel_order):
    panel_cols = match_tiles.shape[0]
    block_share = match_tiles.shape[1]
    row_index = lax.axis_index("prow")
    col_index = lax.axis_index("pcol")
    target = panel_order[col_index]
    whole_cols, normal = gather_pieces_together(match_tiles, True)
    tile_table, column_ids = strip_table(normal)
    product = multiply(
        tile_table, column_ids, pattern, kept, whole_cols, col_index, row_index, block_share
    )
    inflated = product * product
    unused_cols, normal = gather_pieces_together(inflated, False)
    tile_table, column_ids = strip_table(normal)
    target_ids = target * panel_cols + jnp.arange(panel_cols, dtype=jnp.int32)
    target_tiles = tile_table[locate(column_ids, target_ids[None, :])[0]]
    whole_cols = lax.all_gather(target_tiles, "prow", axis=1, tiled=True)
    product = multiply(
        tile_table, column_ids, kept, kept, whole_cols, target, row_index, block_share
    )
    inflated = product * product
    totals = lax.psum(column_partial(inflated), "prow")
    return inflated / totals[:, None, None, :]


def solution(mesh):
    in_specs = (P("pcol", "prow", None, None), P(), P(), P())
    out_specs = P("pcol", "prow", None, None)
    return jax.shard_map(local, mesh=mesh, in_specs=in_specs, out_specs=out_specs, check_vma=False)
```

profile of v0, /device:TPU:0, one launch (start us, length us, event | category | flops | bytes accessed | tf_op | source)
XLA Modules:
  0.0 259.2 jit_solution(4242611748056995517)
XLA Ops:
  6.5 1.1 reduce_sum.78
  7.6 9.5 %all_to_all.15 = f32[4,4,128]{2,1,0:T(4,128)S(1)} all-to-all(f32[4,4,128]{2,1,0:T(4,128)S(1)} %broadcast_in_dim.26), channel_id=1, replica_groups=mesh['prow'=4,'pcol'=32] {'prow'}, dimensions={0} | all-to-all | bytes 16384 | tf_op jit(solution)/shard_map/all_to_all | solution.py:9
  17.2 1.9 broadcast_divide_fusion.2
  19.1 2.6 %broadcast_in_dim.28 = f32[4,4,2,128,128]{4,3,2,1,0:T(8,128)} broadcast(f32[4,2,128,128]{3,2,1,0:T(8,128)} %broadcast_divide_fusion.2), dimensions={1,2,3,4} | broadcast | bytes 2621440 | tf_op jit(solution)/shard_map/broadcast_in_dim | solution.py:9
  21.8 3.6 %all-to-all-start.1 = ((f32[4,4,2,128,128]{4,3,2,1,0:T(8,128)}), f32[4,4,2,128,128]{4,3,2,1,0:T(8,128)S(1)}, u32[]{:S(2)}, u32[]{:S(2)}) async-start(f32[4,4,2,128,128]{4,3,2,1,0:T(8,128)} %broadcast_in_dim.28), calls=%async_computation.1 | async-start | bytes 4194304 | tf_op jit(solution)/shard_map/all_to_all | solution.py:9
  25.5 0.6 dynamic_slice.24
  27.1 0.2 select_reduce_fusion.1
  27.4 0.1 copy.49
  27.5 0.6 gather_fusion.1
  28.2 0.6 gather_fusion.2
  28.8 21.8 %all-to-all-done.1 = f32[4,4,2,128,128]{4,3,2,1,0:T(8,128)S(1)} async-done(((f32[4,4,2,128,128]{4,3,2,1,0:T(8,128)}), f32[4,4,2,128,128]{4,3,2,1,0:T(8,128)S(1)}, u32[]{:S(2)}, u32[]{:S(2)}) %all-to-all-start.1) | async-done | bytes 2097184 | tf_op jit(solution)/shard_map/all_to_all | solution.py:9
  50.5 1.5 copy.32
  52.0 40.5 %all-gather.5.cloned.1.call-done = f32[128,2,128,128]{3,2,1,0:T(8,128)} async-done(((f32[4,2,128,128]{3,2,1,0:T(8,128)}), f32[128,2,128,128]{3,2,1,0:T(8,128)}) %all-gather.5.cloned.1.call-update) | async-done | bytes 16777232 | tf_op jit(solution)/shard_map/all_gather | solution.py:53
  92.5 8.5 %gather_fusion = f32[32,2,128,128]{3,2,1,0:T(8,128)} fusion(f32[128,2,128,128]{3,2,1,0:T(8,128)} %all-gather.5.cloned.1.call-done, s32[1024]{0:T(1024)S(1)} %pad_clamp_fusion.3), kind=kCustom, calls=%fused_computation | custom fusion | bytes 8388736 | tf_op jit(solution)/shard_map/gather | solution.py:66
  101.0 13.6 %fusion.8 = f32[4,2,8,128,128]{4,1,3,2,0:T(2,128)S(1)} fusion(f32[4,8,2,128,128]{4,3,2,1,0:T(8,128)} %bitcast.61, s32[4,2]{1,0:T(4,128)S(1)} %copy.30, s32[4,8,2]{2,1,0:T(8,128)S(1)} %bitcast.65), kind=kOutput, calls=%fused_computation.15 | convolution fusion | flops 25165952 | bytes 8388896 | tf_op jit(solution)/shard_map/jtks,jksab->jtkab/dot_general | solution.py:72
  114.6 3.8 %fusion.42 = (f32[4,128]{1,0:T(4,128)S(1)}, f32[4,2,128,128]{3,2,1,0:T(8,128)S(1)}) fusion(f32[4,8,128,128,1]{3,2,1,4,0:T(8,128)S(1)} %bitcast.64, f32[4,2,8,128,128]{4,1,3,2,0:T(2,128)S(1)} %fusion.8), kind=kOutput, calls=%fused_computation.55 | convolution fusion | flops 1610874368 | bytes 6817792 | tf_op jit(solution)/shard_map/jtkab,jkbc->jtac/dot_general | solution.py:75
  118.4 9.4 %all_to_all.16 = f32[4,4,128]{2,1,0:T(4,128)S(1)} all-to-all(f32[4,4,128]{2,1,0:T(4,128)S(1)} %broadcast_in_dim.29), channel_id=1, replica_groups=mesh['prow'=4,'pcol'=32] {'prow'}, dimensions={0} | all-to-all | bytes 16384 | tf_op jit(solution)/shard_map/all_to_all | solution.py:9
  127.8 0.8 broadcast_divide_fusion.1
  128.7 0.2 all-gather.9.cloned.1.call-start
  128.9 0.2 select_reduce_fusion.2
  129.1 70.0 %all-gather.7.cloned.1.call-done = f32[128,2,128,128]{3,2,1,0:T(8,128)} async-done(((f32[4,2,128,128]{3,2,1,0:T(8,128)}), f32[128,2,128,128]{3,2,1,0:T(8,128)}) %all-gather.7.cloned.1.call-update) | async-done | bytes 16777232 | tf_op jit(solution)/shard_map/all_gather | solution.py:53
  199.1 7.1 %gather_fusion.6 = f32[4,2,128,128]{3,2,1,0:T(8,128)} fusion(f32[128,2,128,128]{3,2,1,0:T(8,128)} %all-gather.7.cloned.1.call-done, s32[1024]{0:T(1024)S(1)} %pad_clamp_fusion), kind=kCustom, calls=%fused_computation.6 | custom fusion | bytes 1048592 | tf_op jit(solution)/shard_map/gather | solution.py:95
  206.5 0.2 select_reduce_fusion
  206.8 0.1 copy.50
  206.9 0.6 gather_fusion.4
  207.6 0.6 gather_fusion.5
  208.2 8.5 %gather_fusion.3 = f32[32,2,128,128]{3,2,1,0:T(8,128)} fusion(f32[128,2,128,128]{3,2,1,0:T(8,128)} %all-gather.7.cloned.1.call-done, s32[1024]{0:T(1024)S(1)} %pad_clamp_fusion.1), kind=kCustom, calls=%fused_computation.3 | custom fusion | bytes 8388736 | tf_op jit(solution)/shard_map/gather | solution.py:66
  216.7 14.7 %fusion.11 = f32[4,2,8,128,128]{4,1,3,2,0:T(2,128)} fusion(f32[4,8,2,128,128]{4,3,2,1,0:T(8,128)} %bitcast.62, s32[4,2]{1,0:T(4,128)S(1)} %copy.38, s32[4,8,2]{2,1,0:T(8,128)S(1)} %bitcast.66), kind=kOutput, calls=%fused_computation.16 | convolution fusion | flops 25165952 | bytes 8388896 | tf_op jit(solution)/shard_map/jtks,jksab->jtkab/dot_general | solution.py:72
  231.4 5.2 %all-gather.9.cloned.1.call-done = f32[4,8,128,128]{3,2,1,0:T(8,128)} async-done(((f32[4,2,128,128]{3,2,1,0:T(8,128)}), f32[4,8,128,128]{3,2,1,0:T(8,128)}) %all-gather.9.cloned.1.call-update) | async-done | bytes 2097168 | tf_op jit(solution)/shard_map/all_gather | solution.py:96
  236.6 6.7 %fusion.43 = (f32[4,128]{1,0:T(4,128)S(1)}, f32[4,2,128,128]{3,2,1,0:T(8,128)S(1)}) fusion(f32[4,8,128,128]{3,2,1,0:T(8,128)} %all-gather.9.cloned.1.call-done, f32[4,2,8,128,128]{4,1,3,2,0:T(2,128)} %fusion.11), kind=kOutput, calls=%fused_computation.56 | convolution fusion | flops 1610874368 | bytes 6817792 | tf_op jit(solution)/shard_map/jtkab,jkbc->jtac/dot_general | solution.py:75
  243.3 8.6 %psum.7 = f32[4,128]{1,0:T(4,128)S(1)} all-reduce(f32[4,128]{1,0:T(4,128)S(1)} %get-tuple-element.9), channel_id=1, replica_groups=mesh['prow'=4,'pcol'=32] {'prow'}, use_global_device_ids=true, to_apply=%region_8.9 | all-reduce | flops 512 | bytes 4096 | tf_op jit(solution)/shard_map/psum | solution.py:101
  251.9 0.8 broadcast_divide_fusion
  (36 shorter events, 1.0 us)
Async XLA Ops:
  6.5 85.9 %all-gather.5.cloned.1.call-start = ((), (), s32[]{:S(2)}) async-start(), calls=%async_computation.3 | async-start | bytes 17301504 | tf_op jit(solution)/shard_map/all_gather | solution.py:53
  17.2 8.3 %copy-start.3 = (s32[32]{0:T(128)S(1)}, s32[32]{0:T(128)}, u32[]{:S(2)}) copy-start(s32[32]{0:T(128)} %param.7) | copy-start | bytes 388
  17.2 9.5 %copy-start.1 = (s32[128,8]{0,1:T(8,128)S(1)}, s32[128,8]{0,1:T(8,128)}, u32[]{:S(2)}) copy-start(s32[128,8]{0,1:T(8,128)} %param.6) | copy-start | bytes 12292
  17.2 9.7 %copy-start.2 = (s32[128,8]{0,1:T(8,128)S(1)}, s32[128,8]{0,1:T(8,128)}, u32[]{:S(2)}) copy-start(s32[128,8]{0,1:T(8,128)} %param.5) | copy-start | bytes 12292
  21.8 28.8 %all-to-all-start.1 = ((f32[4,4,2,128,128]{4,3,2,1,0:T(8,128)}), f32[4,4,2,128,128]{4,3,2,1,0:T(8,128)S(1)}, u32[]{:S(2)}, u32[]{:S(2)}) async-start(f32[4,4,2,128,128]{4,3,2,1,0:T(8,128)} %broadcast_in_dim.28), calls=%async_computation.1 | async-start | bytes 4194304 | tf_op jit(solution)/shard_map/all_to_all | solution.py:9
  25.4 173.7 %all-gather.7.cloned.1.call-start = ((), (), s32[]{:S(2)}) async-start(), calls=%async_computation.4 | async-start | bytes 17301504 | tf_op jit(solution)/shard_map/all_gather | solution.py:53
  101.0 13.6 %copy-start = (f32[4,4,2,128,128]{4,3,2,1,0:T(8,128)S(1)}, f32[4,4,2,128,128]{4,3,2,1,0:T(8,128)}, u32[]{:S(2)}) copy-start(f32[4,4,2,128,128]{4,3,2,1,0:T(8,128)} %copy.32) | copy-start | bytes 6291460
  128.7 107.9 %all-gather.9.cloned.1.call-start = ((), (), s32[]{:S(2)}) async-start(), calls=%async_computation.5 | async-start | bytes 2621440 | tf_op jit(solution)/shard_map/all_gather | solution.py:96
Sparse Core Ops, SparseCore 0:
  19.2 73.1 all-gather.4
  128.8 70.2 all-gather.6
  206.4 30.1 all-gather.8
where the time goes:
time: 260 us; the launch traced here: 259 us
  waiting for transfers between devices  137 us (53%)
  matrix products  38.9 us (15%)
  local copies, waits for them, and re-layouts  32.3 us (12%)
  blocking collectives  27.5 us (11%)
  between operations  13.9 us (5%)
  other arithmetic  5.37 us (2%)
  starting transfers between devices  3.87 us (1%)
    all_gather x2, waiting for transfers between devices, strip_table(): tile_table = lax.all_gather(normal, 'pcol', axis=0, tiled=True)  110 us
    dot_general x2, matrix products, multiply(): jnp.einsum('jtks,jksab->jtkab', weights, needed, precision=lax.Precision....  28.3 us
    all_to_all x1, waiting for transfers between devices, copy_for_each(): lax.all_to_all(jnp.broadcast_to(x[None], (length, *x.shape)), axis, 0, 0,...  21.8 us
    all_to_all x2, blocking collectives, copy_for_each(): lax.all_to_all(jnp.broadcast_to(x[None], (length, *x.shape)), axis, 0, 0,...  18.9 us
    gather x2, local copies, waits for them, and re-layouts, multiply(): needed = tile_table[positions]  17 us
    dot_general x2, matrix products, multiply(): jnp.einsum('jtkab,jkbc->jtac', selected_entries, whole_cols, precision=la...  10.5 us
    psum x1, blocking collectives, local(): totals = lax.psum(column_partial(inflated), 'prow')  8.59 us
    gather x1, local copies, waits for them, and re-layouts, local(): target_tiles = tile_table[locate(column_ids, target_ids[None, :])[0]]  7.14 us
  transfers between devices with their start and end apart: 4, of which 4 were waited for; matrix products, arithmetic and copies ran while one was open for 12% of the time, Pallas kernels for 0%

commit v1 on v0

--- a/solution.py
+++ b/solution.py
@@ -50,7 +50,8 @@
 
 
 def strip_table(normal):
-    tile_table = lax.all_gather(normal, "pcol", axis=0, tiled=True)
+    copies = jnp.concatenate([normal] * lax.axis_size("pcol"), axis=0)
+    tile_table = lax.all_to_all(copies, "pcol", 0, 0, tiled=True)
     column_ids = jnp.arange(tile_table.shape[0], dtype=jnp.int32)
     return (tile_table, column_ids)
 

time: 260 us -> 622 us (2.39)
  waiting for transfers between devices: 137 us -> 435 us
  other arithmetic: 5.37 us -> 31.8 us
  local copies, waits for them, and re-layouts: 32.3 us -> 58 us
  starting transfers between devices: 3.87 us -> 17.5 us
    all_to_all x0 -> x2, waiting for transfers between devices: none -> 421 us  [strip_table(): tile_table = lax.all_to_all(copies, 'pcol', 0, 0, tiled=True)]
    all_gather x2 -> x0, waiting for transfers between devices: 110 us -> none  [strip_table(): tile_table = lax.all_gather(normal, 'pcol', axis=0, tiled=True)]
    unnamed x0 -> x32, other arithmetic: none -> 28.3 us
    unnamed x10 -> x40, local copies, waits for them, and re-layouts: 0.25 us -> 25.6 us
    all_to_all x0 -> x2, starting transfers between devices: none -> 13.8 us  [strip_table(): tile_table = lax.all_to_all(copies, 'pcol', 0, 0, tiled=True)]
    all_to_all x1, waiting for transfers between devices: 21.8 us -> 14.2 us  [copy_for_each(): lax.all_to_all(jnp.broadcast_to(x[None], (length, *x.shape)), axis, 0, 0,...]
  transfers between devices with their start and end apart: 4 -> 4, of which waited for: 4 -> 4; matrix products, arithmetic and copies ran while one was open for 12% -> 7% of each run, Pallas kernels for 0% -> 0%
where the time goes in v1:
time: 622 us; the launch traced here: 621 us
  waiting for transfers between devices  435 us (70%)
  local copies, waits for them, and re-layouts  58 us (9%)
  matrix products  38.8 us (6%)
  other arithmetic  31.8 us (5%)
  blocking collectives  25.8 us (4%)
  starting transfers between devices  17.5 us (3%)
  between operations  14.2 us (2%)
    all_to_all x2, waiting for transfers between devices, strip_table(): tile_table = lax.all_to_all(copies, 'pcol', 0, 0, tiled=True)  421 us
    unnamed x32, other arithmetic  28.3 us
    dot_general x2, matrix products, multiply(): jnp.einsum('jtks,jksab->jtkab', weights, needed, precision=lax.Precision....  28.2 us
    unnamed x40, local copies, waits for them, and re-layouts  25.6 us
    gather x2, local copies, waits for them, and re-layouts, multiply(): needed = tile_table[positions]  17.5 us
    all_to_all x2, blocking collectives, copy_for_each(): lax.all_to_all(jnp.broadcast_to(x[None], (length, *x.shape)), axis, 0, 0,...  17.2 us
    all_to_all x1, waiting for transfers between devices, copy_for_each(): lax.all_to_all(jnp.broadcast_to(x[None], (length, *x.shape)), axis, 0, 0,...  14.2 us
    all_to_all x2, starting transfers between devices, strip_table(): tile_table = lax.all_to_all(copies, 'pcol', 0, 0, tiled=True)  13.8 us
  transfers between devices with their start and end apart: 4, of which 4 were waited for; matrix products, arithmetic and copies ran while one was open for 7% of the time, Pallas kernels for 0%

profile of v1, /device:TPU:0, one launch (start us, length us, event | category | flops | bytes accessed | tf_op | source)
XLA Modules:
  0.0 621.3 jit_solution(6101463635285976835)
XLA Ops:
  6.5 1.1 reduce_sum.78
  7.6 9.5 %all_to_all.25 = f32[4,4,128]{2,1,0:T(4,128)S(1)} all-to-all(f32[4,4,128]{2,1,0:T(4,128)S(1)} %broadcast_in_dim.26), channel_id=1, replica_groups=mesh['prow'=4,'pcol'=32] {'prow'}, dimensions={0} | all-to-all | bytes 16384 | tf_op jit(solution)/shard_map/all_to_all | solution.py:9
  17.2 1.9 constant_dynamic-update-slice_fusion.31
  31.8 0.9 constant_dynamic-update-slice_fusion.15
  32.7 0.9 constant_dynamic-update-slice_fusion.14
  34.4 1.6 broadcast_in_dim.28
  36.0 3.6 all-to-all-start.2
  40.4 0.9 constant_dynamic-update-slice_fusion.11
  44.7 0.9 constant_dynamic-update-slice_fusion.6
  50.6 14.2 %all-to-all-done.2 = f32[4,4,2,128,128]{4,3,2,1,0:T(8,128)S(1)} async-done(((f32[4,4,2,128,128]{4,3,2,1,0:T(8,128)}), f32[4,4,2,128,128]{4,3,2,1,0:T(8,128)S(1)}, u32[]{:S(2)}, u32[]{:S(2)}) %all-to-all-start.2) | async-done | bytes 2097184 | tf_op jit(solution)/shard_map/all_to_all | solution.py:9
  64.7 8.6 %all-to-all-start.1 = ((f32[128,2,128,128]{3,2,1,0:T(8,128)}), f32[128,2,128,128]{3,2,1,0:T(8,128)}, u32[]{:S(2)}, u32[]{:S(2)}) async-start(f32[128,2,128,128]{3,2,1,0:T(8,128)} %constant_dynamic-update-slice_fusion), calls=%async_computation.1 | async-start | bytes 33554432 | tf_op jit(solution)/shard_map/all_to_all | solution.py:54
  76.7 1.5 copy.32
  78.1 208.3 %all-to-all-done.1 = f32[128,2,128,128]{3,2,1,0:T(8,128)} async-done(((f32[128,2,128,128]{3,2,1,0:T(8,128)}), f32[128,2,128,128]{3,2,1,0:T(8,128)}, u32[]{:S(2)}, u32[]{:S(2)}) %all-to-all-start.1) | async-done | bytes 16777248 | tf_op jit(solution)/shard_map/all_to_all | solution.py:54
  286.5 8.5 %gather_fusion = f32[32,2,128,128]{3,2,1,0:T(8,128)} fusion(f32[128,2,128,128]{3,2,1,0:T(8,128)} %all-to-all-done.1, s32[1024]{0:T(1024)S(1)} %pad_clamp_fusion.3), kind=kCustom, calls=%fused_computation | custom fusion | bytes 8388736 | tf_op jit(solution)/shard_map/gather | solution.py:67
  295.0 13.5 %fusion.8 = f32[4,2,8,128,128]{4,1,3,2,0:T(2,128)S(1)} fusion(f32[4,8,2,128,128]{4,3,2,1,0:T(8,128)} %bitcast.61, s32[4,2]{1,0:T(4,128)S(1)} %copy.30, s32[4,8,2]{2,1,0:T(8,128)S(1)} %bitcast.65), kind=kOutput, calls=%fused_computation.15 | convolution fusion | flops 25165952 | bytes 8388896 | tf_op jit(solution)/shard_map/jtks,jksab->jtkab/dot_general | solution.py:73
  308.4 3.9 fusion.42
  312.3 7.7 %all_to_all.26 = f32[4,4,128]{2,1,0:T(4,128)S(1)} all-to-all(f32[4,4,128]{2,1,0:T(4,128)S(1)} %broadcast_in_dim.29), channel_id=1, replica_groups=mesh['prow'=4,'pcol'=32] {'prow'}, dimensions={0} | all-to-all | bytes 16384 | tf_op jit(solution)/shard_map/all_to_all | solution.py:9
  322.5 0.9 constant_dynamic-update-slice_fusion.60
  327.6 0.9 constant_dynamic-update-slice_fusion.54
  331.0 0.9 constant_dynamic-update-slice_fusion.50
  333.6 0.9 constant_dynamic-update-slice_fusion.47
  334.5 0.9 constant_dynamic-update-slice_fusion.46
  337.0 0.9 constant_dynamic-update-slice_fusion.43
  340.4 0.9 constant_dynamic-update-slice_fusion.39
  341.3 0.9 constant_dynamic-update-slice_fusion.38
  347.2 5.2 all-to-all-start.4
  353.1 212.6 %all-to-all-done.4 = f32[128,2,128,128]{3,2,1,0:T(8,128)} async-done(((f32[128,2,128,128]{3,2,1,0:T(8,128)}), f32[128,2,128,128]{3,2,1,0:T(8,128)}, u32[]{:S(2)}, u32[]{:S(2)}) %all-to-all-start.4) | async-done | bytes 16777248 | tf_op jit(solution)/shard_map/all_to_all | solution.py:54
  565.7 7.1 %gather_fusion.6 = f32[4,2,128,128]{3,2,1,0:T(8,128)} fusion(f32[128,2,128,128]{3,2,1,0:T(8,128)} %all-to-all-done.4, s32[1024]{0:T(1024)S(1)} %get-tuple-element.15), kind=kCustom, calls=%fused_computation.6 | custom fusion | bytes 1048592 | tf_op jit(solution)/shard_map/gather | solution.py:96
  574.3 9.0 %gather_fusion.3 = f32[32,2,128,128]{3,2,1,0:T(8,128)} fusion(f32[128,2,128,128]{3,2,1,0:T(8,128)} %all-to-all-done.4, s32[1024]{0:T(1024)S(1)} %get-tuple-element.16), kind=kCustom, calls=%fused_computation.3 | custom fusion | bytes 8388736 | tf_op jit(solution)/shard_map/gather | solution.py:67
  583.3 14.8 %fusion.11 = f32[4,2,8,128,128]{4,1,3,2,0:T(2,128)} fusion(f32[4,8,2,128,128]{4,3,2,1,0:T(8,128)} %bitcast.62, s32[4,2]{1,0:T(4,128)S(1)} %copy.38, s32[4,8,2]{2,1,0:T(8,128)S(1)} %bitcast.66), kind=kOutput, calls=%fused_computation.16 | convolution fusion | flops 25165952 | bytes 8388896 | tf_op jit(solution)/shard_map/jtks,jksab->jtkab/dot_general | solution.py:73
  598.3 6.7 %fusion.43 = (f32[4,128]{1,0:T(4,128)S(1)}, f32[4,2,128,128]{3,2,1,0:T(8,128)S(1)}) fusion(f32[4,8,128,128]{3,2,1,0:T(8,128)} %all-gather.3.cloned.1.call-done, f32[4,2,8,128,128]{4,1,3,2,0:T(2,128)} %fusion.11), kind=kOutput, calls=%fused_computation.120 | convolution fusion | flops 1610874368 | bytes 6817792 | tf_op jit(solution)/shard_map/jtkab,jkbc->jtac/dot_general | solution.py:76
  605.0 8.6 %psum.7 = f32[4,128]{1,0:T(4,128)S(1)} all-reduce(f32[4,128]{1,0:T(4,128)S(1)} %get-tuple-element.11), channel_id=1, replica_groups=mesh['prow'=4,'pcol'=32] {'prow'}, use_global_device_ids=true, to_apply=%region_8.9 | all-reduce | flops 512 | bytes 4096 | tf_op jit(solution)/shard_map/psum | solution.py:102
  (95 shorter events, 48.7 us)
Async XLA Ops:
  36.0 28.8 %all-to-all-start.2 = ((f32[4,4,2,128,128]{4,3,2,1,0:T(8,128)}), f32[4,4,2,128,128]{4,3,2,1,0:T(8,128)S(1)}, u32[]{:S(2)}, u32[]{:S(2)}) async-start(f32[4,4,2,128,128]{4,3,2,1,0:T(8,128)} %broadcast_in_dim.28), calls=%async_computation.2 | async-start | bytes 4194304 | tf_op jit(solution)/shard_map/all_to_all | solution.py:9
  50.5 22.8 %copy-start.3 = (s32[32]{0:T(128)S(1)}, s32[32]{0:T(128)}, u32[]{:S(2)}) copy-start(s32[32]{0:T(128)} %param.7) | copy-start | bytes 388
  50.6 24.1 %copy-start.2 = (s32[128,8]{0,1:T(8,128)S(1)}, s32[128,8]{0,1:T(8,128)}, u32[]{:S(2)}) copy-start(s32[128,8]{0,1:T(8,128)} %param.5) | copy-start | bytes 12292
  50.6 24.6 %copy-start.1 = (s32[128,8]{0,1:T(8,128)S(1)}, s32[128,8]{0,1:T(8,128)}, u32[]{:S(2)}) copy-start(s32[128,8]{0,1:T(8,128)} %param.6) | copy-start | bytes 12292
  64.7 221.7 %all-to-all-start.1 = ((f32[128,2,128,128]{3,2,1,0:T(8,128)}), f32[128,2,128,128]{3,2,1,0:T(8,128)}, u32[]{:S(2)}, u32[]{:S(2)}) async-start(f32[128,2,128,128]{3,2,1,0:T(8,128)} %constant_dynamic-update-slice_fusion), calls=%async_computation.1 | async-start | bytes 33554432 | tf_op jit(solution)/shard_map/all_to_all | solution.py:54
  78.1 230.3 %copy-start = (f32[4,4,2,128,128]{4,3,2,1,0:T(8,128)S(1)}, f32[4,4,2,128,128]{4,3,2,1,0:T(8,128)}, u32[]{:S(2)}) copy-start(f32[4,4,2,128,128]{4,3,2,1,0:T(8,128)} %copy.32) | copy-start | bytes 6291460
  347.2 218.5 %all-to-all-start.4 = ((f32[128,2,128,128]{3,2,1,0:T(8,128)}), f32[128,2,128,128]{3,2,1,0:T(8,128)}, u32[]{:S(2)}, u32[]{:S(2)}) async-start(f32[128,2,128,128]{3,2,1,0:T(8,128)} %constant_dynamic-update-slice_fusion.32), calls=%async_computation.4 | async-start | bytes 33554432 | tf_op jit(solution)/shard_map/all_to_all | solution.py:54
  352.4 245.9 %all-gather.3.cloned.1.call-start = ((), (), s32[]{:S(2)}) async-start(), calls=%async_computation.5 | async-start | bytes 2621440 | tf_op jit(solution)/shard_map/all_gather | solution.py:97
Sparse Core Ops, SparseCore 0:
  573.0 25.2 all-gather.2
